TPU v7x, 32 devices: a whole 2x2x4 slice. The times are simulated.
32 devices in a mesh: dp: 4 (over x, core), fsdp: 8 (over z, y).
Axes of the slice: x: 2, y: 2, z: 4, core: 2. Of those that a mesh axis runs over, the one named last changes fastest.
Arguments:
- frames: bfloat16 [8, 1024, 1024], P('fsdp', 'dp'), may hold values from -6 to 6
- cotangent: bfloat16 [8, 1024, 1024], P('fsdp', 'dp'), may hold values from -6 to 6
- phon_len: int32 [8], replicated, may hold values from 32 to 128
- acou_len: int32 [8], replicated, may hold values from 128 to 895
- row_item: int32 [8], P('fsdp'), may hold values from 0 to 7, each once
- w_qkv: bfloat16 [1024, 3072], P(('dp', 'fsdp')), may hold values from -0.1875 to 0.1875
- w_out: bfloat16 [1024, 1024], P(('dp', 'fsdp')), may hold values from -2 to 2
- w_up: bfloat16 [1024, 4096], P(('dp', 'fsdp')), may hold values from -0.1875 to 0.1875
- w_down: bfloat16 [4096, 1024], P(('dp', 'fsdp')), may hold values from -0.09375 to 0.09375
- ln1_gain: bfloat16 [1024], P(('dp', 'fsdp')), may hold values from 0.25 to 1.75
- ln1_bias: bfloat16 [1024], P(('dp', 'fsdp')), may hold values from -2.5 to 2.5
- ln2_gain: bfloat16 [1024], P(('dp', 'fsdp')), may hold values from 0.25 to 1.75
- ln2_bias: bfloat16 [1024], P(('dp', 'fsdp')), may hold values from -2.5 to 2.5
Outputs:
- activations: bfloat16 [8, 1024, 1024], P('fsdp', 'dp')
- input_grad: float32 [8, 1024, 1024], P('fsdp', 'dp')
- w_qkv_grad: float32 [1024, 3072], P(('dp', 'fsdp'))
- w_out_grad: float32 [1024, 1024], P(('dp', 'fsdp'))
- w_up_grad: float32 [1024, 4096], P(('dp', 'fsdp'))
- w_down_grad: float32 [4096, 1024], P(('dp', 'fsdp'))
- ln1_gain_grad: float32 [1024], P(('dp', 'fsdp'))
- ln1_bias_grad: float32 [1024], P(('dp', 'fsdp'))
- ln2_gain_grad: float32 [1024], P(('dp', 'fsdp'))
- ln2_bias_grad: float32 [1024], P(('dp', 'fsdp'))
Inputs may be any that keep to these rules, and one draw needn't show every extreme that they name: `acou_len`: an item's phoneme and acoustic lengths together are under 1024. `row_item`: each row holds a different item.
All inputs are finite; a program needn't handle non-finite values.
Results may differ from a plain program's by a relative error of at most 0.011.
Values may be sent and summed in bfloat16 or wider, within the bound.
A program may use at most 256 MiB of HBM per device.

v0:
```python
import jax
import jax.numpy as jnp
from jax import lax
from jax.sharding import PartitionSpec as P

HEADS = 16
HEAD_DIM = 64


epsilon = 1e-05
masked_out = -1e30


def layer_norm(vector, gain_vec, bias_vec):
    row_mean = jnp.mean(vector, axis=-1, keepdims=True)
    centered = vector - row_mean
    row_var = jnp.mean(centered * centered, axis=-1, keepdims=True)
    return centered * lax.rsqrt(row_var + epsilon) * gain_vec + bias_vec


def split_heads(matrix):
    return matrix.reshape(matrix.shape[0], HEADS, HEAD_DIM).transpose(1, 0, 2)


def join_heads(tensor):
    return tensor.transpose(1, 0, 2).reshape(tensor.shape[1], HEADS * HEAD_DIM)


def on_device(
    frames,
    cotangent,
    phon_len,
    acou_len,
    row_item,
    w_qkv,
    w_out,
    w_up,
    w_down,
    ln1_gain,
    ln1_bias,
    ln2_gain,
    ln2_bias,
):
    f32 = jnp.float32
    bf16 = jnp.bfloat16
    gathered = (
        lax.all_gather(w_qkv, ("dp", "fsdp"), axis=0, tiled=True),
        lax.all_gather(w_out, ("dp", "fsdp"), axis=0, tiled=True),
        lax.all_gather(w_up, ("dp", "fsdp"), axis=0, tiled=True),
        lax.all_gather(w_down, ("dp", "fsdp"), axis=0, tiled=True),
        lax.all_gather(ln1_gain, ("dp", "fsdp"), axis=0, tiled=True),
        lax.all_gather(ln1_bias, ("dp", "fsdp"), axis=0, tiled=True),
        lax.all_gather(ln2_gain, ("dp", "fsdp"), axis=0, tiled=True),
        lax.all_gather(ln2_bias, ("dp", "fsdp"), axis=0, tiled=True),
    )
    proj_qkv, proj_out, proj_up, proj_down, gain_one, bias_one, gain_two, bias_two = gathered
    gain_one = gain_one.astype(f32)
    bias_one = bias_one.astype(f32)
    gain_two = gain_two.astype(f32)
    bias_two = bias_two.astype(f32)
    seg_len = frames.shape[1]
    model_width = frames.shape[2]
    span = seg_len * lax.axis_size("dp")
    score_scale = HEAD_DIM ** (-0.5)
    item_now = row_item[0]
    matches = jnp.arange(phon_len.shape[0], dtype=jnp.int32) == item_now
    phon_count = jnp.sum(jnp.where(matches, phon_len, 0))
    acou_count = jnp.sum(jnp.where(matches, acou_len, 0))
    row_pos = lax.axis_index("dp") * seg_len + jnp.arange(seg_len, dtype=jnp.int32)
    key_pos = jnp.arange(span, dtype=jnp.int32)
    allowed = (key_pos[None, :] < phon_count) | (key_pos[None, :] >= phon_count) & (
        key_pos[None, :] <= row_pos[:, None]
    ) & (row_pos[:, None] < phon_count + acou_count)
    inputs = frames[0].astype(f32)
    normed1 = layer_norm(inputs, gain_one, bias_one).astype(bf16)
    qkv = jnp.dot(normed1, proj_qkv, preferred_element_type=f32).astype(bf16)
    query = qkv[:, :model_width]
    key_local = qkv[:, model_width : 2 * model_width]
    value_local = qkv[:, 2 * model_width :]
    keys_all, values_all = (
        lax.all_gather(key_local, "dp", axis=0, tiled=True),
        lax.all_gather(value_local, "dp", axis=0, tiled=True),
    )
    q_heads = split_heads(query)
    k_heads = split_heads(keys_all)
    v_heads = split_heads(values_all)

    def head_forward(pieces):
        q_head, k_head, v_head = pieces
        scores = jnp.dot(q_head, k_head.T, preferred_element_type=f32) * score_scale
        scores = jnp.where(allowed, scores, masked_out)
        row_max = jnp.max(scores, axis=-1, keepdims=True)
        exponent = jnp.exp(scores - row_max)
        row_total = jnp.sum(exponent, axis=-1, keepdims=True)
        prob_low = (exponent / row_total).astype(bf16)
        head_out = jnp.dot(prob_low, v_head, preferred_element_type=f32)
        return (head_out, (row_max + jnp.log(row_total))[:, 0])

    head_out, log_total = lax.map(head_forward, (q_heads, k_heads, v_heads))
    attn_out = join_heads(head_out).astype(bf16)
    middle = inputs + jnp.dot(attn_out, proj_out, preferred_element_type=f32)
    normed2 = layer_norm(middle, gain_two, bias_two).astype(bf16)
    up_out = jnp.dot(normed2, proj_up, preferred_element_type=f32)
    act_out = jax.nn.gelu(up_out, approximate=False).astype(bf16)
    result = (middle + jnp.dot(act_out, proj_down, preferred_element_type=f32)).astype(bf16)
    back_qkv, back_out, back_up, back_down, back_gain1, back_gain2 = (
        lax.all_gather(w_qkv, ("dp", "fsdp"), axis=0, tiled=True),
        lax.all_gather(w_out, ("dp", "fsdp"), axis=0, tiled=True),
        lax.all_gather(w_up, ("dp", "fsdp"), axis=0, tiled=True),
        lax.all_gather(w_down, ("dp", "fsdp"), axis=0, tiled=True),
        lax.all_gather(ln1_gain, ("dp", "fsdp"), axis=0, tiled=True),
        lax.all_gather(ln2_gain, ("dp", "fsdp"), axis=0, tiled=True),
    )
    back_gain1 = back_gain1.astype(f32)
    back_gain2 = back_gain2.astype(f32)
    grad_out = cotangent[0].astype(f32)
    grad_down = grad_out.astype(bf16)
    grad_w_down = jnp.dot(act_out.T, grad_down, preferred_element_type=f32)
    grad_act = jnp.dot(grad_down, back_down.T, preferred_element_type=f32)
    _, gelu_back = jax.vjp(lambda pre_act: jax.nn.gelu(pre_act, approximate=False), up_out)
    grad_up = gelu_back(grad_act)[0].astype(bf16)
    grad_w_up = jnp.dot(normed2.T, grad_up, preferred_element_type=f32)
    grad_norm2 = jnp.dot(grad_up, back_up.T, preferred_element_type=f32)
    _, norm_back2 = jax.vjp(layer_norm, middle, back_gain2, bias_two)
    grad_mid_norm, grad_gain2, grad_bias2 = norm_back2(grad_norm2)
    grad_middle = grad_out + grad_mid_norm
    grad_proj = grad_middle.astype(bf16)
    grad_w_out = jnp.dot(attn_out.T, grad_proj, preferred_element_type=f32)
    grad_attn = jnp.dot(grad_proj, back_out.T, preferred_element_type=f32).astype(bf16)
    grad_heads = split_heads(grad_attn)

    def head_backward(pieces):
        q_head, k_head, v_head, g_head, lse_head = pieces
        scores = jnp.dot(q_head, k_head.T, preferred_element_type=f32) * score_scale
        scores = jnp.where(allowed, scores, masked_out)
        probs = jnp.exp(scores - lse_head[:, None])
        grad_probs = jnp.dot(g_head, v_head.T, preferred_element_type=f32)
        grad_value = jnp.dot(probs.astype(bf16).T, g_head, preferred_element_type=f32)
        delta = jnp.sum(probs * grad_probs, axis=-1, keepdims=True)
        grad_scores = (probs * (grad_probs - delta)).astype(bf16)
        grad_query = jnp.dot(grad_scores, k_head, preferred_element_type=f32) * score_scale
        grad_key = jnp.dot(grad_scores.T, q_head, preferred_element_type=f32) * score_scale
        return (grad_query, grad_key, grad_value)

    grad_query, grad_key, grad_value = lax.map(
        head_backward, (q_heads, k_heads, v_heads, grad_heads, log_total)
    )
    key_grad, value_grad = (
        lax.psum_scatter(join_heads(grad_key), "dp", scatter_dimension=0, tiled=True),
        lax.psum_scatter(join_heads(grad_value), "dp", scatter_dimension=0, tiled=True),
    )
    grad_qkv = jnp.concatenate(
        [join_heads(grad_query).astype(bf16), key_grad.astype(bf16), value_grad.astype(bf16)],
        axis=1,
    )
    grad_w_qkv = jnp.dot(normed1.T, grad_qkv, preferred_element_type=f32)
    grad_norm1 = jnp.dot(grad_qkv, back_qkv.T, preferred_element_type=f32)
    _, norm_back1 = jax.vjp(layer_norm, inputs, back_gain1, bias_one)
    grad_in_norm, grad_gain1, grad_bias1 = norm_back1(grad_norm1)
    grad_inputs = grad_middle + grad_in_norm
    owned = (
        lax.psum_scatter(grad_w_qkv, ("dp", "fsdp"), scatter_dimension=0, tiled=True),
        lax.psum_scatter(grad_w_out, ("dp", "fsdp"), scatter_dimension=0, tiled=True),
        lax.psum_scatter(grad_w_up, ("dp", "fsdp"), scatter_dimension=0, tiled=True),
        lax.psum_scatter(grad_w_down, ("dp", "fsdp"), scatter_dimension=0, tiled=True),
        lax.psum_scatter(grad_gain1, ("dp", "fsdp"), scatter_dimension=0, tiled=True),
        lax.psum_scatter(grad_bias1, ("dp", "fsdp"), scatter_dimension=0, tiled=True),
        lax.psum_scatter(grad_gain2, ("dp", "fsdp"), scatter_dimension=0, tiled=True),
        lax.psum_scatter(grad_bias2, ("dp", "fsdp"), scatter_dimension=0, tiled=True),
    )
    return (
        result[None],
        grad_inputs[None],
        owned[0],
        owned[1],
        owned[2],
        owned[3],
        owned[4],
        owned[5],
        owned[6],
        owned[7],
    )


def solution(mesh):
    return jax.shard_map(
        on_device,
        mesh=mesh,
        in_specs=(
            P("fsdp", "dp", None),
            P("fsdp", "dp", None),
            P(),
            P(),
            P("fsdp"),
            P(("dp", "fsdp"), None),
            P(("dp", "fsdp"), None),
            P(("dp", "fsdp"), None),
            P(("dp", "fsdp"), None),
            P(("dp", "fsdp")),
            P(("dp", "fsdp")),
            P(("dp", "fsdp")),
            P(("dp", "fsdp")),
        ),
        out_specs=(
            P("fsdp", "dp", None),
            P("fsdp", "dp", None),
            P(("dp", "fsdp"), None),
            P(("dp", "fsdp"), None),
            P(("dp", "fsdp"), None),
            P(("dp", "fsdp"), None),
            P(("dp", "fsdp")),
            P(("dp", "fsdp")),
            P(("dp", "fsdp")),
            P(("dp", "fsdp")),
        ),
        check_vma=False,
    )
```

profile of v0, /device:TPU:0, one launch (start us, length us, event | category | flops | bytes accessed | tf_op | source)
XLA Modules:
  0.0 1632.9 jit_solution(13206246939249008416)
XLA Ops:
  11.3 42.4 %all-reduce.9 = (bf16[1024]{0:T(1024)(128)(2,1)S(1)}, bf16[1024]{0:T(1024)(128)(2,1)S(1)}, bf16[1024]{0:T(1024)(128)(2,1)S(1)}, bf16[1024]{0:T(1024)(128)(2,1)S(1)}) all-reduce(bf16[1024]{0:T(1024)(128)(2,1)S(1)} %dynamic-update-slice.1, bf16[1024]{0:T(1024)(128)(2,1)S(1)} %dynamic-update-slice, ...), channel_id=1, replica_groups=mesh['dp'=4,'fsdp'=8] {'dp','fsdp'}, use_global_device_ids=true, to_apply=%add.1 | all-reduce | flops 4096 | bytes 16384
  56.3 26.7 %all-gather.7.cloned.1.call-done = bf16[1024,3072]{1,0:T(8,128)(2,1)} async-done(((bf16[32,3072]{1,0:T(8,128)(2,1)}), bf16[1024,3072]{1,0:T(8,128)(2,1)}) %all-gather.7.cloned.1.call-update) | async-done | bytes 6291472 | tf_op jit(solution)/shard_map/all_gather | solution.py:47
  83.0 4.9 convolution_convert_fusion
  97.0 13.2 all-gather.9.cloned.1.call-done
  110.2 2.9 copy.39
  113.1 3.2 copy.42
  116.3 18.7 %all-gather.11.cloned.1.call-done = bf16[1024,1024]{1,0:T(8,128)(2,1)} async-done(((bf16[256,1024]{1,0:T(8,128)(2,1)}), bf16[1024,1024]{1,0:T(8,128)(2,1)}) %all-gather.11.cloned.1.call-update) | async-done | bytes 2097168 | tf_op jit(solution)/shard_map/all_gather | solution.py:82
  135.0 2.9 copy.40
  137.8 3.2 copy.43
  141.1 52.6 %while.28 = (s32[]{:T(128)}, bf16[16,256,64]{1,2,0:T(8,128)(2,1)S(1)}, f32[16,256]{1,0:T(8,128)S(1)}, bf16[16,256,64]{2,1,0:T(8,128)(2,1)}, bf16[16,1024,64]{2,1...) while((s32[]{:T(128)}, ...), condition=%wide.region_7.8_spmd.clone, body=%wide.region_4.7_spmd.clone.sunk | while | flops 70254336 | bytes 3816833 | solution.py:99
  194.3 2.4 fusion.97
  197.0 76.2 %all-gather.15.cloned.1.call-done = bf16[1024,4096]{1,0:T(8,128)(2,1)} async-done(((bf16[32,4096]{1,0:T(8,128)(2,1)}), bf16[1024,4096]{1,0:T(8,128)(2,1)}) %all-gather.15.cloned.1.call-update) | async-done | bytes 8388624 | tf_op jit(solution)/shard_map/all_gather | solution.py:49
  273.2 15.8 multiply_convert_fusion.1
  288.9 62.8 %all-gather.17.cloned.1.call-done = bf16[4096,1024]{1,0:T(8,128)(2,1)} async-done(((bf16[128,1024]{1,0:T(8,128)(2,1)}), bf16[4096,1024]{1,0:T(8,128)(2,1)}) %all-gather.17.cloned.1.call-update) | async-done | bytes 8388624 | tf_op jit(solution)/shard_map/all_gather | solution.py:50
  351.8 11.6 add_convert_fusion
  363.4 2.7 multiply_reduce_fusion.1
  369.3 2.0 copy.44
  372.2 136.6 %while.29 = (s32[]{:T(128)}, bf16[16,256,64]{1,2,0:T(8,128)(2,1)}, f32[16,1024,64]{1,2,0:T(8,128)}, f32[16,1024,64]{1,2,0:T(8,128)}, bf16[16,256,64]{2,1,0:T(8,1...) while((s32[]{:T(128)}, bf16[16,256,64]{1,2,0:T(8,128)(2,1)}, ...), condition=%wide.region_14.15_spmd.clone, body=%wide.region_12.14_spmd.clone.sunk | while | flops 171261696 | bytes 9450897 | solution.py:145
  375.4 1.9 fusion.146
  383.9 1.9 fusion.146
  392.4 1.9 fusion.146
  400.9 1.9 fusion.146
  409.5 1.9 fusion.146
  418.1 1.9 fusion.146
  419.9 1.8 fusion.147
  426.6 1.9 fusion.146
  435.1 1.9 fusion.146
  443.7 1.9 fusion.146
  452.2 1.9 fusion.146
  460.8 1.9 fusion.146
  469.3 1.9 fusion.146
  477.9 1.9 fusion.146
  486.4 1.9 fusion.146
  494.9 1.9 fusion.146
  503.4 1.9 fusion.146
  509.6 3.9 fusion.98
  513.5 38.5 %reduce-scatter.9.cloned.1.call-done = f32[256,1024]{0,1:T(8,128)} async-done(((f32[1024,1024]{0,1:T(8,128)}), f32[256,1024]{0,1:T(8,128)}) %reduce-scatter.9.cloned.1.call-update) | async-done | bytes 1048592 | tf_op jit(solution)/shard_map/reduce_scatter | solution.py:150
  553.3 45.7 %reduce-scatter.7.cloned.1.call-done = f32[256,1024]{0,1:T(8,128)} async-done(((f32[1024,1024]{0,1:T(8,128)}), f32[256,1024]{0,1:T(8,128)}) %reduce-scatter.7.cloned.1.call-update) | async-done | bytes 1048592 | tf_op jit(solution)/shard_map/reduce_scatter | solution.py:149
  601.0 7.6 fusion.73
  608.7 9.8 fusion.90
  619.5 9.7 fusion.75
  629.3 7.3 fusion.64
  636.6 4.8 fusion.92
  641.9 41.1 %all-reduce.8 = (f32[1024]{0:T(1024)S(1)}, f32[1024]{0:T(1024)S(1)}, f32[1024]{0:T(1024)S(1)}, f32[1024]{0:T(1024)S(1)}) all-reduce(f32[1024]{0:T(1024)S(1)} %get-tuple-element.213, f32[1024]{0:T(1024)S(1)} %get-tuple-element.216, f32[1024]{0:T(1024)S(1)} %get-tuple-element.211, ...), channel_id=8, replica_groups=mesh['dp'=4,'fsdp'=8] {'dp','fsdp'}, use_global_device_ids=true, to_apply=%region_24.25.clone | all-reduce | flops 4096 | bytes 32768
  686.8 60.4 %reduce-scatter.13.cloned.1.call-done = f32[32,1024]{1,0:T(8,128)} async-done(((f32[1024,1024]{1,0:T(8,128)}), f32[32,1024]{1,0:T(8,128)}) %reduce-scatter.13.cloned.1.call-update) | async-done | bytes 131088 | tf_op jit(solution)/shard_map/reduce_scatter | solution.py:163
  747.1 158.8 %reduce-scatter.11.cloned.1.call-done = f32[32,3072]{1,0:T(8,128)} async-done(((f32[1024,3072]{1,0:T(8,128)}), f32[32,3072]{1,0:T(8,128)}) %reduce-scatter.11.cloned.1.call-update) | async-done | bytes 393232 | tf_op jit(solution)/shard_map/reduce_scatter | solution.py:162
  905.9 360.0 %reduce-scatter.15.cloned.1.call-done = f32[32,4096]{1,0:T(8,128)} async-done(((f32[1024,4096]{1,0:T(8,128)}), f32[32,4096]{1,0:T(8,128)}) %reduce-scatter.15.cloned.1.call-update) | async-done | bytes 524304 | tf_op jit(solution)/shard_map/reduce_scatter | solution.py:164
  1265.9 360.1 %reduce-scatter.17.cloned.1.call-done = f32[128,1024]{1,0:T(8,128)} async-done(((f32[4096,1024]{1,0:T(8,128)}), f32[128,1024]{1,0:T(8,128)}) %reduce-scatter.17.cloned.1.call-update) | async-done | bytes 524304 | tf_op jit(solution)/shard_map/reduce_scatter | solution.py:165
  (277 shorter events, 184.9 us)
Async XLA Ops:
  7.2 75.8 %all-gather.7.cloned.1.call-start = ((), (), s32[]{:S(2)}) async-start(), calls=%async_computation.6 | async-start | bytes 6488064 | tf_op jit(solution)/shard_map/all_gather | solution.py:47
  7.9 102.3 %all-gather.9.cloned.1.call-start = ((), (), s32[]{:S(2)}) async-start(), calls=%async_computation.7 | async-start | bytes 2621440 | tf_op jit(solution)/shard_map/all_gather | solution.py:81
  87.9 4.4 copy-start.13
  87.9 5.7 copy-start.14
  89.0 46.0 %all-gather.11.cloned.1.call-start = ((), (), s32[]{:S(2)}) async-start(), calls=%async_computation.8 | async-start | bytes 2621440 | tf_op jit(solution)/shard_map/all_gather | solution.py:82
  89.7 104.6 %all-gather.13.cloned.1.call-start = ((), (), s32[]{:S(2)}) async-start(), calls=%async_computation.9 | async-start | bytes 2162688 | tf_op jit(solution)/shard_map/all_gather | solution.py:48
  90.3 182.9 %all-gather.15.cloned.1.call-start = ((), (), s32[]{:S(2)}) async-start(), calls=%async_computation.10 | async-start | bytes 8650752 | tf_op jit(solution)/shard_map/all_gather | solution.py:49
  90.9 260.9 %all-gather.17.cloned.1.call-start = ((), (), s32[]{:S(2)}) async-start(), calls=%async_computation.11 | async-start | bytes 8650752 | tf_op jit(solution)/shard_map/all_gather | solution.py:50
  91.5 460.5 %reduce-scatter.9.cloned.1.call-start = ((), (), s32[]{:S(2)}) async-start(), calls=%async_computation.13 | async-start | bytes 5242880 | tf_op jit(solution)/shard_map/reduce_scatter | solution.py:150
  141.1 53.2 %copy-start = (bf16[1,256,1024]{2,1,0:T(8,128)(2,1)S(1)}, bf16[1,256,1024]{2,1,0:T(8,128)(2,1)}, u32[]{:S(2)}) copy-start(bf16[1,256,1024]{2,1,0:T(8,128)(2,1)} %param.17) | copy-start | bytes 1572868
  197.0 154.7 %copy-start.1 = (bf16[1,256,1024]{2,1,0:T(8,128)(2,1)S(1)}, bf16[1,256,1024]{2,1,0:T(8,128)(2,1)}, u32[]{:S(2)}) copy-start(bf16[1,256,1024]{2,1,0:T(8,128)(2,1)} %param.18) | copy-start | bytes 1572868
  351.8 11.6 copy-start.12
  363.4 2.7 copy-start.11
  363.4 3.2 copy-start.2
  366.1 1.6 copy-start.8
  366.8 0.8 copy-start.10
  508.8 90.1 %reduce-scatter.7.cloned.1.call-start = ((), (), s32[]{:S(2)}) async-start(), calls=%async_computation.12 | async-start | bytes 5242880 | tf_op jit(solution)/shard_map/reduce_scatter | solution.py:149
  509.5 237.6 %reduce-scatter.13.cloned.1.call-start = ((), (), s32[]{:S(2)}) async-start(), calls=%async_computation.15 | async-start | bytes 4325376 | tf_op jit(solution)/shard_map/reduce_scatter | solution.py:163
  513.5 392.4 %reduce-scatter.11.cloned.1.call-start = ((), (), s32[]{:S(2)}) async-start(), calls=%async_computation.14 | async-start | bytes 12976128 | tf_op jit(solution)/shard_map/reduce_scatter | solution.py:162
  553.3 55.3 %copy-start.4 = (bf16[256,1024]{0,1:T(8,128)(2,1)}, bf16[256,1024]{0,1:T(8,128)(2,1)S(1)}, u32[]{:S(2)}) copy-start(bf16[256,1024]{0,1:T(8,128)(2,1)S(1)} %convert_element_type.103) | copy-start | bytes 1572868
  600.2 0.8 copy-start.6
  608.6 657.3 %reduce-scatter.15.cloned.1.call-start = ((), (), s32[]{:S(2)}) async-start(), calls=%async_computation.16 | async-start | bytes 17301504 | tf_op jit(solution)/shard_map/reduce_scatter | solution.py:164
  618.5 1.0 copy-start.3
  618.5 1007.5 %reduce-scatter.17.cloned.1.call-start = ((), (), s32[]{:S(2)}) async-start(), calls=%async_computation.17 | async-start | bytes 17301504 | tf_op jit(solution)/shard_map/reduce_scatter | solution.py:165
  629.3 7.3 copy-start.5
  629.3 7.3 copy-start.7
  629.3 7.3 copy-start.9
Sparse Core Ops, SparseCore 0:
  10.9 72.0 all-gather.6
  89.1 21.0 all-gather.8
  112.4 22.5 all-gather.10
  137.8 56.4 all-gather.12
  197.1 75.9 all-gather.14
  276.0 75.6 all-gather.16
  508.9 43.0 reduce-scatter.8
  554.5 44.3 reduce-scatter.6
  601.8 145.3 reduce-scatter.12
  753.6 152.2 reduce-scatter.10
  908.8 357.1 reduce-scatter.14
  1268.7 357.3 reduce-scatter.16
where the time goes:
time: 1640 us; the launch traced here: 1630 us
  waiting for transfers between devices  1230 us (75%)
  matrix products  262 us (16%)
  blocking collectives  83.5 us (5%)
  local copies, waits for them, and re-layouts  26.8 us (2%)
  other arithmetic  17.5 us (1%)
  between operations  16.5 us (1%)
    reduce_scatter x1, waiting for transfers between devices, on_device(): lax.psum_scatter(grad_w_down, ('dp', 'fsdp'), scatter_dimension=0, tiled=...  360 us
    reduce_scatter x1, waiting for transfers between devices, on_device(): lax.psum_scatter(grad_w_up, ('dp', 'fsdp'), scatter_dimension=0, tiled=True)  360 us
    reduce_scatter x1, waiting for transfers between devices, on_device(): lax.psum_scatter(grad_w_qkv, ('dp', 'fsdp'), scatter_dimension=0, tiled=T...  159 us
    unnamed x2, blocking collectives  83.5 us
    all_gather x1, waiting for transfers between devices, on_device(): lax.all_gather(w_up, ('dp', 'fsdp'), axis=0, tiled=True)  76.2 us
    all_gather x1, waiting for transfers between devices, on_device(): lax.all_gather(w_down, ('dp', 'fsdp'), axis=0, tiled=True)  62.8 us
    reduce_scatter x1, waiting for transfers between devices, on_device(): lax.psum_scatter(grad_w_out, ('dp', 'fsdp'), scatter_dimension=0, tiled=T...  60.4 us
    reduce_scatter x1, waiting for transfers between devices, on_device(): lax.psum_scatter(join_heads(grad_key), 'dp', scatter_dimension=0, tiled=T...  45.7 us
  transfers between devices with their start and end apart: 12, of which 12 were waited for; matrix products, arithmetic and copies ran while one was open for 9% of the time, Pallas kernels for 0%

commit v1 on v0

v1 whole, which is shorter than its diff:
```python
import functools

import jax
import jax.numpy as jnp
from jax import lax
from jax.experimental import pallas as pl
from jax.experimental.pallas import tpu as pltpu
from jax.sharding import PartitionSpec as P

HEAD_DIM = 64
EPS = 1e-05
MASKED = -1e30
BLOCK = 256

f32 = jnp.float32
bf16 = jnp.bfloat16


def dot(a, b, ca, cb):
    return lax.dot_general(a, b, (((ca,), (cb,)), ((), ())), preferred_element_type=f32)


def row_limit(start, rows, phon, acou):
    pos = start + lax.broadcasted_iota(jnp.int32, (1, rows), 1)
    return jnp.where(pos < phon + acou, jnp.maximum(pos, phon - 1), phon - 1)


def head_mask(width, head):
    lane = lax.broadcasted_iota(jnp.int32, (1, width), 1)
    return (lane >= head * HEAD_DIM) & (lane < (head + 1) * HEAD_DIM)


def attn_fwd_kernel(lens, qkv, out, lse):
    width = out.shape[1]
    heads = width // HEAD_DIM
    length = out.shape[0]
    phon, acou = lens[0], lens[1]
    scale = HEAD_DIM ** (-0.5)
    for start in range(0, length, BLOCK):
        seen = start + BLOCK
        q = qkv[start : start + BLOCK, :width] * scale
        k = qkv[:seen, width : 2 * width]
        v = qkv[:seen, 2 * width :]
        limit = row_limit(start, BLOCK, phon, acou)
        key = lax.broadcasted_iota(jnp.int32, (seen, 1), 0)
        hidden = key > limit
        total = jnp.zeros((BLOCK, width), f32)
        rows = []
        for h in range(heads):
            mine = head_mask(width, h)
            qh = jnp.where(mine, q, 0)
            s = dot(k, qh, 1, 1)
            s = jnp.where(hidden, MASKED, s)
            top = jnp.max(s, axis=0, keepdims=True)
            e = jnp.exp(s - top)
            tot = jnp.sum(e, axis=0, keepdims=True)
            p = (e * (1.0 / tot)).astype(bf16)
            o = dot(p, v, 0, 0)
            total = total + jnp.where(mine, o, 0)
            rows.append(top + jnp.log(tot))
        out[start : start + BLOCK, :] = total.astype(bf16)
        lse[:, start : start + BLOCK] = jnp.concatenate(rows + [jnp.zeros((8 - heads, BLOCK), f32)], axis=0)


def attn_bwd_kernel(lens, qkv, grad, lse, dqkv, dk_acc, dv_acc):
    width = grad.shape[1]
    heads = width // HEAD_DIM
    length = grad.shape[0]
    phon, acou = lens[0], lens[1]
    scale = HEAD_DIM ** (-0.5)
    for start in reversed(range(0, length, BLOCK)):
        seen = start + BLOCK
        q = qkv[start : start + BLOCK, :width] * scale
        g = grad[start : start + BLOCK, :]
        k = qkv[:seen, width : 2 * width]
        v = qkv[:seen, 2 * width :]
        limit = row_limit(start, BLOCK, phon, acou)
        key = lax.broadcasted_iota(jnp.int32, (seen, 1), 0)
        hidden = key > limit
        dq = jnp.zeros((BLOCK, width), f32)
        for h in range(heads):
            mine = head_mask(width, h)
            qh = jnp.where(mine, q, 0)
            gh = jnp.where(mine, g, 0)
            s = dot(k, qh, 1, 1)
            s = jnp.where(hidden, MASKED, s)
            p = jnp.exp(s - lse[h : h + 1, start : start + BLOCK])
            gp = dot(v, gh, 1, 1)
            delta = jnp.sum(p * gp, axis=0, keepdims=True)
            ds = (p * (gp - delta)).astype(bf16)
            dvh = dot(p.astype(bf16), gh, 1, 0)
            dkh = dot(ds, qh, 1, 0)
            if start == length - BLOCK and h == 0:
                dv_acc[...] = dvh
                dk_acc[...] = dkh
            else:
                dv_acc[:seen, :] += dvh
                dk_acc[:seen, :] += dkh
            dq = dq + jnp.where(mine, dot(ds, k, 0, 0), 0)
        dqkv[start : start + BLOCK, :width] = (dq * scale).astype(bf16)
    dqkv[:, width : 2 * width] = dk_acc[...].astype(bf16)
    dqkv[:, 2 * width :] = dv_acc[...].astype(bf16)


VMEM = pl.BlockSpec(memory_space=pltpu.VMEM)
SMEM = pl.BlockSpec(memory_space=pltpu.SMEM)


def attn_fwd(lens, qkv):
    length, width = qkv.shape[0], qkv.shape[1] // 3
    return pl.pallas_call(
        attn_fwd_kernel,
        out_shape=(jax.ShapeDtypeStruct((length, width), bf16), jax.ShapeDtypeStruct((8, length), f32)),
        in_specs=[SMEM, VMEM],
        out_specs=(VMEM, VMEM),
        compiler_params=pltpu.CompilerParams(vmem_limit_bytes=40 * 2**20),
        cost_estimate=pl.CostEstimate(flops=4 * length * length * width, bytes_accessed=8 * length * width, transcendentals=length * length * width // HEAD_DIM),
        name="attn_fwd",
    )(lens, qkv)


def attn_bwd(lens, qkv, grad, lse):
    length, width = grad.shape
    return pl.pallas_call(
        attn_bwd_kernel,
        out_shape=jax.ShapeDtypeStruct((length, 3 * width), bf16),
        in_specs=[SMEM, VMEM, VMEM, VMEM],
        out_specs=VMEM,
        scratch_shapes=[pltpu.VMEM((length, width), f32), pltpu.VMEM((length, width), f32)],
        compiler_params=pltpu.CompilerParams(vmem_limit_bytes=40 * 2**20),
        cost_estimate=pl.CostEstimate(flops=10 * length * length * width, bytes_accessed=14 * length * width, transcendentals=length * length * width // HEAD_DIM),
        name="attn_bwd",
    )(lens, qkv, grad, lse)


def norm_parts(v):
    mean = jnp.mean(v, axis=-1, keepdims=True)
    centered = v - mean
    var = jnp.mean(centered * centered, axis=-1, keepdims=True)
    inv = lax.rsqrt(var + EPS)
    return centered * inv, inv


def norm_back(n, inv, gain, grad):
    g = grad * gain
    dx = inv * (g - jnp.mean(g, axis=-1, keepdims=True) - n * jnp.mean(g * n, axis=-1, keepdims=True))
    return dx, jnp.sum(grad * n, axis=0), jnp.sum(grad, axis=0)


def on_device(frames, cotangent, phon_len, acou_len, row_item, w_qkv, w_out, w_up, w_down, ln1_gain, ln1_bias, ln2_gain, ln2_bias):
    tp, dpn, fsn = "dp", lax.axis_size("dp"), lax.axis_size("fsdp")
    width = frames.shape[2]
    part = width // dpn
    rows = w_up.shape[0]

    vecs = jnp.concatenate([ln1_gain, ln1_bias, ln2_gain, ln2_bias])[None]
    vecs = lax.all_gather(vecs, ("dp", "fsdp"), axis=0, tiled=True)
    vecs = vecs.reshape(dpn * fsn, 4, rows).transpose(1, 0, 2).reshape(4, width).astype(f32)

    qkv_cols = w_qkv.reshape(rows, 3, dpn, part).transpose(2, 0, 1, 3).reshape(dpn, rows, 3 * part)
    qkv_cols = lax.all_to_all(qkv_cols, tp, 0, 0, tiled=True)
    wq = lax.all_gather(qkv_cols, "fsdp", axis=1, tiled=True).reshape(width, 3 * part)
    wo = lax.all_gather(w_out, "fsdp", axis=0, tiled=True)
    ff = w_up.shape[1] // dpn
    up_cols = w_up.reshape(rows, dpn, ff).transpose(1, 0, 2)
    up_cols = lax.all_to_all(up_cols, tp, 0, 0, tiled=True)
    wu = lax.all_gather(up_cols, "fsdp", axis=1, tiled=True).reshape(width, ff)
    wd = lax.all_gather(w_down, "fsdp", axis=0, tiled=True)

    item = row_item[0]
    pick = jnp.arange(phon_len.shape[0], dtype=jnp.int32) == item
    lens = jnp.stack([jnp.sum(jnp.where(pick, phon_len, 0)), jnp.sum(jnp.where(pick, acou_len, 0))])

    x = frames[0].astype(f32)
    n1, inv1 = norm_parts(x)
    normed1 = lax.all_gather((n1 * vecs[0] + vecs[1]).astype(bf16), tp, axis=0, tiled=True)
    grad_down = lax.all_gather(cotangent[0], tp, axis=0, tiled=True)
    qkv = jnp.dot(normed1, wq, preferred_element_type=f32).astype(bf16)
    attn_out, lse = attn_fwd(lens, qkv)
    proj = jnp.dot(attn_out, wo, preferred_element_type=f32).astype(bf16)
    middle = x + lax.psum_scatter(proj, tp, scatter_dimension=0, tiled=True).astype(f32)
    n2, inv2 = norm_parts(middle)
    normed2 = lax.all_gather((n2 * vecs[2] + vecs[3]).astype(bf16), tp, axis=0, tiled=True)
    up_out = jnp.dot(normed2, wu, preferred_element_type=f32)
    cdf = 0.5 * (1.0 + lax.erf(up_out * (0.5**0.5)))
    act_out = (up_out * cdf).astype(bf16)
    down = jnp.dot(act_out, wd, preferred_element_type=f32).astype(bf16)
    result = (middle + lax.psum_scatter(down, tp, scatter_dimension=0, tiled=True).astype(f32)).astype(bf16)

    g_down = dot(act_out, grad_down, 0, 0).astype(bf16)
    slope = cdf + up_out * (jnp.exp(-0.5 * up_out * up_out) * (1.0 / (2.0 * jnp.pi) ** 0.5))
    grad_up = (dot(grad_down, wd, 1, 1) * slope).astype(bf16)
    g_up = dot(normed2, grad_up, 0, 0).astype(bf16)
    grad_norm2 = lax.psum_scatter(dot(grad_up, wu, 1, 1).astype(bf16), tp, scatter_dimension=0, tiled=True).astype(f32)
    mid_norm, g_gain2, g_bias2 = norm_back(n2, inv2, vecs[2], grad_norm2)
    grad_middle = cotangent[0].astype(f32) + mid_norm
    grad_proj = lax.all_gather(grad_middle.astype(bf16), tp, axis=0, tiled=True)
    g_out = dot(attn_out, grad_proj, 0, 0).astype(bf16)
    grad_attn = dot(grad_proj, wo, 1, 1).astype(bf16)
    grad_qkv = attn_bwd(lens, qkv, grad_attn, lse)
    g_qkv = dot(normed1, grad_qkv, 0, 0).astype(bf16)
    grad_norm1 = lax.psum_scatter(dot(grad_qkv, wq, 1, 1).astype(bf16), tp, scatter_dimension=0, tiled=True).astype(f32)
    in_norm, g_gain1, g_bias1 = norm_back(n1, inv1, vecs[0], grad_norm1)
    grad_inputs = grad_middle + in_norm

    def owned_rows(g):
        return lax.psum_scatter(g, "fsdp", scatter_dimension=0, tiled=True)

    def owned_cols(g, groups):
        g = lax.psum_scatter(g.reshape(dpn, width // dpn, -1), "fsdp", scatter_dimension=1, tiled=True)
        g = lax.all_to_all(g, tp, 0, 0, tiled=True)
        g = g.reshape(dpn, rows, groups, -1).transpose(1, 2, 0, 3)
        return g.reshape(rows, -1).astype(f32)

    o_down = owned_rows(g_down).astype(f32)
    o_up = owned_cols(g_up, 1)
    o_out = owned_rows(g_out).astype(f32)
    o_qkv = owned_cols(g_qkv, 3)
    small = jnp.stack([g_gain1, g_bias1, g_gain2, g_bias2]).reshape(4, dpn * fsn, rows).transpose(1, 0, 2)
    small = lax.psum_scatter(small.reshape(dpn * fsn, 4 * rows), ("dp", "fsdp"), scatter_dimension=0, tiled=True).reshape(4, rows)
    return (result[None], grad_inputs[None], o_qkv, o_out, o_up, o_down, small[0], small[1], small[2], small[3])


def solution(mesh):
    split = P(("dp", "fsdp"), None)
    vec = P(("dp", "fsdp"))
    acts = P("fsdp", "dp", None)
    return jax.shard_map(
        on_device,
        mesh=mesh,
        in_specs=(acts, acts, P(), P(), P("fsdp"), split, split, split, split, vec, vec, vec, vec),
        out_specs=(acts, acts, split, split, split, split, vec, vec, vec, vec),
        check_vma=False,
    )
```

time: 1640 us -> 752 us (0.46)
  waiting for transfers between devices: 1230 us -> 458 us
  matrix products: 262 us -> 54.6 us
  blocking collectives: 83.5 us -> 157 us
  Pallas kernels: 0 us -> 16.8 us
    reduce_scatter x6 -> x8, waiting for transfers between devices: 1020 us -> 313 us  [the longest x2 128 us: owned_rows(): return lax.psum_scatter(g, 'fsdp', scatter_dimension=0, tiled=True)]
    dot_general x124 -> x12, matrix products: 262 us -> 54.6 us  [the longest x8 35.8 us: dot(): lax.dot_general(a, b, (((ca,), (cb,)), ((), ())), preferred_element_type=...]
    all_gather x0 -> x2, blocking collectives: none -> 99.4 us  [the longest x1 67.8 us: on_device(): vecs = lax.all_gather(vecs, ('dp', 'fsdp'), axis=0, tiled=True)]
    all_gather x6 -> x7, waiting for transfers between devices: 198 us -> 144 us  [the longest x1 51.2 us: on_device(): wd = lax.all_gather(w_down, 'fsdp', axis=0, tiled=True)]
    unnamed x2 -> x1, blocking collectives: 83.5 us -> 39.4 us
    all_to_all x0 -> x2, blocking collectives: none -> 17.9 us  [the longest x1 9.44 us: on_device(): qkv_cols = lax.all_to_all(qkv_cols, tp, 0, 0, tiled=True)]
    pallas_call x0 -> x2, Pallas kernels: none -> 16.8 us  [the longest x1 11 us: attn_bwd(): pl.pallas_call(attn_bwd_kernel, out_shape=jax.ShapeDtypeStruct((length, 3...]
  transfers between devices with their start and end apart: 12 -> 17, of which waited for: 12 -> 12; matrix products, arithmetic and copies ran while one was open for 9% -> 8% of each run, Pallas kernels for 0% -> 1%
where the time goes in v1:
time: 752 us; the launch traced here: 743 us
  waiting for transfers between devices  458 us (61%)
  blocking collectives  157 us (21%)
  matrix products  54.6 us (7%)
  other arithmetic  20.5 us (3%)
  Pallas kernels  16.8 us (2%)
  between operations  15.4 us (2%)
  local copies, waits for them, and re-layouts  13.5 us (2%)
  starting transfers between devices  7.77 us (1%)
    reduce_scatter x2, waiting for transfers between devices, owned_rows(): return lax.psum_scatter(g, 'fsdp', scatter_dimension=0, tiled=True)  128 us
    reduce_scatter x2, waiting for transfers between devices, owned_cols(): lax.psum_scatter(g.reshape(dpn, width // dpn, -1), 'fsdp', scatter_dimens...  107 us
    all_gather x1, blocking collectives, on_device(): vecs = lax.all_gather(vecs, ('dp', 'fsdp'), axis=0, tiled=True)  67.8 us
    all_gather x1, waiting for transfers between devices, on_device(): wd = lax.all_gather(w_down, 'fsdp', axis=0, tiled=True)  51.2 us
    all_gather x1, waiting for transfers between devices, on_device(): wu = lax.all_gather(up_cols, 'fsdp', axis=1, tiled=True).reshape(width, ff)  46.3 us
    unnamed x1, blocking collectives  39.4 us
    dot_general x8, matrix products, dot(): lax.dot_general(a, b, (((ca,), (cb,)), ((), ())), preferred_element_type=...  35.8 us
    all_gather x1, blocking collectives, on_device(): wo = lax.all_gather(w_out, 'fsdp', axis=0, tiled=True)  31.6 us
  transfers between devices with their start and end apart: 17, of which 12 were waited for; matrix products, arithmetic and copies ran while one was open for 8% of the time, Pallas kernels for 1%

profile of v1, /device:TPU:0, one launch (start us, length us, event | category | flops | bytes accessed | tf_op | source)
XLA Modules:
  0.0 743.2 jit_solution(4916770478501427309)
XLA Ops:
  7.2 1.1 reshape.128
  8.7 9.4 %all_to_all.20 = bf16[4,32,768]{2,1,0:T(8,128)(2,1)} all-to-all(bf16[4,32,768]{2,1,0:T(8,128)(2,1)S(1)} %reshape.129), channel_id=1, replica_groups=mesh['dp'=4,'fsdp'=8] {'dp'}, dimensions={0} | all-to-all | bytes 393216 | tf_op jit(solution)/shard_map/all_to_all | solution.py:161
  19.0 67.8 %all-gather.2 = bf16[32,1,128]{2,1,0:T(2,128)(2,1)S(1)} all-gather(bf16[1,1,128]{2,1,0:T(2,128)(2,1)S(1)} %maximum_bitcast_fusion.1), channel_id=2, replica_groups=mesh['dp'=4,'fsdp'=8] {'dp','fsdp'}, dimensions={0}, use_global_device_ids=true | all-gather | bytes 8448 | tf_op jit(solution)/shard_map/all_gather | solution.py:157
  90.2 1.4 pad_add_fusion.lens
  91.6 31.6 %all_gather.30 = bf16[256,1024]{1,0:T(8,128)(2,1)S(1)} all-gather(bf16[32,1024]{1,0:T(8,128)(2,1)S(1)} %copy-done.9), channel_id=1, replica_groups=mesh['dp'=4,'fsdp'=8] {'fsdp'}, dimensions={0}, use_global_device_ids=true | all-gather | bytes 589824 | tf_op jit(solution)/shard_map/all_gather | solution.py:163
  123.2 4.0 convolution_convert_fusion.6.qkv
  127.2 5.8 attn_fwd.1
  133.0 2.1 convolution_convert_fusion.3
  135.4 8.5 %all_to_all.21 = bf16[4,32,1024]{2,1,0:T(8,128)(2,1)S(1)} all-to-all(bf16[4,32,1024]{2,1,0:T(8,128)(2,1)S(1)} %copy.32), channel_id=1, replica_groups=mesh['dp'=4,'fsdp'=8] {'dp'}, dimensions={0} | all-to-all | bytes 524288 | tf_op jit(solution)/shard_map/all_to_all | solution.py:166
  145.0 18.5 %reduce-scatter.9.cloned.1.call-done = bf16[256,1024]{1,0:T(8,128)(2,1)} async-done(((bf16[1024,1024]{1,0:T(8,128)(2,1)}), bf16[256,1024]{1,0:T(8,128)(2,1)}) %reduce-scatter.9.cloned.1.call-update) | async-done | bytes 524304 | tf_op jit(solution)/shard_map/reduce_scatter | solution.py:181
  163.5 1.3 fusion.38
  164.9 1.3 multiply_reduce_fusion
  166.2 1.1 add_convert_fusion.1
  168.9 46.3 %all-gather.17.cloned.1.call-done = bf16[4,256,1024]{2,0,1:T(4,128)(2,1)} async-done(((bf16[4,32,1024]{2,0,1:T(4,128)(2,1)}), bf16[4,256,1024]{2,0,1:T(4,128)(2,1)}) %all-gather.17.cloned.1.call-update) | async-done | bytes 2097168 | tf_op jit(solution)/shard_map/all_gather | solution.py:167
  215.2 3.6 copy.34
  218.8 19.6 %all-gather.15.cloned.1.call-done = bf16[1024,1024]{1,0:T(8,128)(2,1)} async-done(((bf16[256,1024]{1,0:T(8,128)(2,1)}), bf16[1024,1024]{1,0:T(8,128)(2,1)}) %all-gather.15.cloned.1.call-update) | async-done | bytes 2097168 | tf_op jit(solution)/shard_map/all_gather | solution.py:183
  238.3 7.5 %multiply_convert_fusion = (bf16[1024,1024]{1,0:T(8,128)(2,1)}, f32[1024,1024]{1,0:T(8,128)}) fusion(bf16[1024,1024]{1,0:T(8,128)(2,1)} %all-gather.15.cloned.1.call-done, bf16[1024,1024]{1,0:T(8,128)(2,1)} %bitcast.133), kind=kOutput, calls=%fused_computation.7 | convolution fusion | flops 2152726528 | bytes 10485760 | tf_op jit(solution)/shard_map/dot_general | solution.py:184
  245.8 16.5 %all-gather.23.cloned.1.call-done = bf16[1,1024,1024]{2,1,0:T(8,128)(2,1)} async-done(((bf16[1,256,1024]{2,1,0:T(8,128)(2,1)}), bf16[1,1024,1024]{2,1,0:T(8,128)(2,1)}) %all-gather.23.cloned.1.call-update) | async-done | bytes 2097168 | tf_op jit(solution)/shard_map/all_gather | solution.py:177
  262.3 51.2 %all-gather.19.cloned.1.call-done = bf16[1024,1024]{1,0:T(8,128)(2,1)} async-done(((bf16[128,1024]{1,0:T(8,128)(2,1)}), bf16[1024,1024]{1,0:T(8,128)(2,1)}) %all-gather.19.cloned.1.call-update) | async-done | bytes 2097168 | tf_op jit(solution)/shard_map/all_gather | solution.py:168
  313.6 6.3 fusion.5
  319.9 1.3 copy-done.14
  321.2 3.7 convolution_convert_fusion.1
  325.0 29.8 %reduce-scatter.13.cloned.1.call-done = bf16[256,1024]{1,0:T(8,128)(2,1)} async-done(((bf16[1024,1024]{1,0:T(8,128)(2,1)}), bf16[256,1024]{1,0:T(8,128)(2,1)}) %reduce-scatter.13.cloned.1.call-update) | async-done | bytes 524304 | tf_op jit(solution)/shard_map/reduce_scatter | solution.py:194
  354.8 1.6 fusion.36
  356.5 2.5 fusion.42
  359.1 6.0 convolution_convert_fusion
  365.1 6.3 fusion.9
  371.7 10.1 %all-gather.21.cloned.1.call-done = bf16[1024,1024]{1,0:T(8,128)(2,1)} async-done(((bf16[256,1024]{1,0:T(8,128)(2,1)}), bf16[1024,1024]{1,0:T(8,128)(2,1)}) %all-gather.21.cloned.1.call-update) | async-done | bytes 2097168 | tf_op jit(solution)/shard_map/all_gather | solution.py:197
  381.8 2.4 convolution_convert_fusion.8.grad
  384.2 11.0 %attn_bwd.1 = bf16[1024,768]{1,0:T(8,128)(2,1)S(1)} custom-call(s32[2]{0:T(128)S(1)} %pad_add_fusion.lens, bf16[1024,768]{1,0:T(8,128)(2,1)S(1)} %convolution_convert_fusion.6.qkv, bf16[1024,256]{1,0:T(8,128)(2,1)S(1)} %convolution_convert_fusion.8.grad, f32[8,1024]{1,0:T(8,128)S(1)} %get-tuple-element.13.lse), custom_call_target="tpu_custom_call" | custom-call | flops 2684354560 | bytes 3670016 | tf_op jit(solution)/shard_map/attn_bwd/pallas_call | solution.py:124
  395.3 3.3 convolution_convert_fusion.5
  398.6 3.2 convolution_convert_fusion.7
  402.0 4.6 convolution_convert_fusion.4
  406.6 1.6 copy-done.13
  408.2 5.3 convolution_convert_fusion.2
  413.5 40.6 %reduce-scatter.21.cloned.1.call-done = bf16[4,32,1024]{2,1,0:T(8,128)(2,1)} async-done(((bf16[4,256,1024]{2,1,0:T(8,128)(2,1)}), bf16[4,32,1024]{2,1,0:T(8,128)(2,1)}) %reduce-scatter.21.cloned.1.call-update) | async-done | bytes 262160 | tf_op jit(solution)/shard_map/reduce_scatter | solution.py:210
  454.0 3.4 all-to-all-start.3
  457.6 67.4 %reduce-scatter.23.cloned.1.call-done = bf16[128,1024]{1,0:T(8,128)(2,1)} async-done(((bf16[1024,1024]{1,0:T(8,128)(2,1)}), bf16[128,1024]{1,0:T(8,128)(2,1)}) %reduce-scatter.23.cloned.1.call-update) | async-done | bytes 262160 | tf_op jit(solution)/shard_map/reduce_scatter | solution.py:207
  525.0 1.8 convert_element_type.144
  526.8 66.2 %reduce-scatter.17.cloned.1.call-done = bf16[4,32,768]{2,1,0:T(8,128)(2,1)} async-done(((bf16[4,256,768]{2,1,0:T(8,128)(2,1)}), bf16[4,32,768]{2,1,0:T(8,128)(2,1)}) %reduce-scatter.17.cloned.1.call-update) | async-done | bytes 196624 | tf_op jit(solution)/shard_map/reduce_scatter | solution.py:210
  593.0 3.4 all-to-all-start.2
  596.7 1.1 copy.37
  597.8 60.7 %reduce-scatter.19.cloned.1.call-done = bf16[32,1024]{1,0:T(8,128)(2,1)} async-done(((bf16[256,1024]{1,0:T(8,128)(2,1)}), bf16[32,1024]{1,0:T(8,128)(2,1)}) %reduce-scatter.19.cloned.1.call-update) | async-done | bytes 65552 | tf_op jit(solution)/shard_map/reduce_scatter | solution.py:207
  658.6 1.5 convert_element_type.137
  661.5 29.6 %reduce-scatter.15.cloned.1.call-done = bf16[256,1024]{1,0:T(8,128)(2,1)} async-done(((bf16[1024,1024]{1,0:T(8,128)(2,1)}), bf16[256,1024]{1,0:T(8,128)(2,1)}) %reduce-scatter.15.cloned.1.call-update) | async-done | bytes 524304 | tf_op jit(solution)/shard_map/reduce_scatter | solution.py:202
  691.1 1.6 fusion.37
  693.1 39.4 %all-reduce = f32[32,128]{1,0:T(8,128)S(1)} all-reduce(f32[32,128]{1,0:T(8,128)S(1)} %reshape.135), channel_id=12, replica_groups=mesh['dp'=4,'fsdp'=8] {'dp','fsdp'}, use_global_device_ids=true, to_apply=%region_22.23.clone | all-reduce | flops 4096 | bytes 32768
  733.1 3.2 fusion.29
  (101 shorter events, 10.5 us)
Async XLA Ops:
  7.2 80.1 %copy-start.2 = (bf16[1,256,1024]{2,1,0:T(8,128)(2,1)S(1)}, bf16[1,256,1024]{2,1,0:T(8,128)(2,1)}, u32[]{:S(2)}) copy-start(bf16[1,256,1024]{2,1,0:T(8,128)(2,1)} %param.13) | copy-start | bytes 1572868
  7.2 116.0 %all-gather.13.cloned.1.call-start = ((), (), s32[]{:S(2)}) async-start(), calls=%async_computation.13 | async-start | bytes 1769472 | tf_op jit(solution)/shard_map/all_gather | solution.py:162
  8.5 81.1 %copy-start.10 = (s32[8]{0:T(128)S(1)}, s32[8]{0:T(128)}, u32[]{:S(2)}) copy-start(s32[8]{0:T(128)} %param.15) | copy-start | bytes 100
  8.5 81.1 %copy-start.11 = (s32[8]{0:T(128)S(1)}, s32[8]{0:T(128)}, u32[]{:S(2)}) copy-start(s32[8]{0:T(128)} %param.16) | copy-start | bytes 100
  8.5 83.1 %copy-start.9 = (bf16[32,1024]{1,0:T(8,128)(2,1)S(1)}, bf16[32,1024]{1,0:T(8,128)(2,1)}, u32[]{:S(2)}) copy-start(bf16[32,1024]{1,0:T(8,128)(2,1)} %param.19) | copy-start | bytes 196612
  18.2 105.0 %all-gather.11.cloned.1.call-start = ((), (), s32[]{:S(2)}) async-start(), calls=%async_computation.12 | async-start | bytes 2621440 | tf_op jit(solution)/shard_map/all_gather | solution.py:176
  88.9 74.7 %reduce-scatter.9.cloned.1.call-start = ((), (), s32[]{:S(2)}) async-start(), calls=%async_computation.14 | async-start | bytes 2621440 | tf_op jit(solution)/shard_map/reduce_scatter | solution.py:181
  123.2 9.8 %copy-start.7 = (bf16[256,1024]{1,0:T(8,128)(2,1)}, bf16[256,1024]{1,0:T(8,128)(2,1)S(1)}, u32[]{:S(2)}) copy-start(bf16[256,1024]{1,0:T(8,128)(2,1)S(1)} %all_gather.30) | copy-start | bytes 1572868
  133.0 2.2 copy-start.8
  135.1 80.2 %all-gather.17.cloned.1.call-start = ((), (), s32[]{:S(2)}) async-start(), calls=%async_computation.16 | async-start | bytes 2359296 | tf_op jit(solution)/shard_map/all_gather | solution.py:167
  144.8 93.5 %all-gather.15.cloned.1.call-start = ((), (), s32[]{:S(2)}) async-start(), calls=%async_computation.15 | async-start | bytes 2621440 | tf_op jit(solution)/shard_map/all_gather | solution.py:183
  163.5 2.7 copy-start.3
  167.3 95.0 %all-gather.23.cloned.1.call-start = ((), (), s32[]{:S(2)}) async-start(), calls=%async_computation.26 | async-start | bytes 2621440 | tf_op jit(solution)/shard_map/all_gather | solution.py:177
  167.9 145.7 %all-gather.19.cloned.1.call-start = ((), (), s32[]{:S(2)}) async-start(), calls=%async_computation.17 | async-start | bytes 2359296 | tf_op jit(solution)/shard_map/all_gather | solution.py:168
  168.7 186.2 %reduce-scatter.13.cloned.1.call-start = ((), (), s32[]{:S(2)}) async-start(), calls=%async_computation.19 | async-start | bytes 2621440 | tf_op jit(solution)/shard_map/reduce_scatter | solution.py:194
  313.6 7.6 %copy-start.6 = (bf16[4,256,1024]{2,1,0:T(8,128)(2,1)S(1)}, bf16[4,256,1024]{2,1,0:T(8,128)(2,1)}, u32[]{:S(2)}) copy-start(bf16[4,256,1024]{2,1,0:T(8,128)(2,1)} %copy.34) | copy-start | bytes 6291460
  319.9 1.3 copy-start.14
  325.0 56.8 %all-gather.21.cloned.1.call-start = ((), (), s32[]{:S(2)}) async-start(), calls=%async_computation.20 | async-start | bytes 2621440 | tf_op jit(solution)/shard_map/all_gather | solution.py:197
  359.1 95.0 %reduce-scatter.21.cloned.1.call-start = ((), (), s32[]{:S(2)}) async-start(), calls=%async_computation.24 | async-start | bytes 2359296 | tf_op jit(solution)/shard_map/reduce_scatter | solution.py:210
  365.1 159.9 %reduce-scatter.23.cloned.1.call-start = ((), (), s32[]{:S(2)}) async-start(), calls=%async_computation.25 | async-start | bytes 2359296 | tf_op jit(solution)/shard_map/reduce_scatter | solution.py:207
  371.4 221.5 %reduce-scatter.17.cloned.1.call-start = ((), (), s32[]{:S(2)}) async-start(), calls=%async_computation.22 | async-start | bytes 1769472 | tf_op jit(solution)/shard_map/reduce_scatter | solution.py:210
  384.2 11.1 %copy-start.12 = (bf16[1024,1024]{1,0:T(8,128)(2,1)S(1)}, bf16[1024,1024]{1,0:T(8,128)(2,1)}, u32[]{:S(2)}) copy-start(bf16[1024,1024]{1,0:T(8,128)(2,1)} %all-gather.11.cloned.1.call-done) | copy-start | bytes 6291460
  395.3 3.3 copy-start
  398.6 3.4 copy-start.1
  398.6 260.0 %reduce-scatter.19.cloned.1.call-start = ((), (), s32[]{:S(2)}) async-start(), calls=%async_computation.23 | async-start | bytes 589824 | tf_op jit(solution)/shard_map/reduce_scatter | solution.py:207
  401.9 289.2 %reduce-scatter.15.cloned.1.call-start = ((), (), s32[]{:S(2)}) async-start(), calls=%async_computation.21 | async-start | bytes 2621440 | tf_op jit(solution)/shard_map/reduce_scatter | solution.py:202
  406.6 1.7 copy-start.13
  406.6 326.5 %reduce-scatter.11.cloned.1.call-start = ((), (), s32[]{:S(2)}) async-start(), calls=%async_computation.18 | async-start | bytes 2621440 | tf_op jit(solution)/shard_map/reduce_scatter | solution.py:188
  454.0 72.7 %all-to-all-start.3 = ((bf16[4,32,1024]{2,1,0:T(8,128)(2,1)}), bf16[4,32,1024]{2,1,0:T(8,128)(2,1)S(1)}, u32[]{:S(2)}, u32[]{:S(2)}) async-start(bf16[4,32,1024]{2,1,0:T(8,128)(2,1)} %reduce-scatter.21.cloned.1.call-done), calls=%async_computation.10 | async-start | bytes 524288 | tf_op jit(solution)/shard_map/all_to_all | solution.py:211
  593.0 67.1 %all-to-all-start.2 = ((bf16[4,32,768]{2,1,0:T(8,128)(2,1)}), bf16[4,32,768]{2,1,0:T(8,128)(2,1)S(1)}, u32[]{:S(2)}, u32[]{:S(2)}) async-start(bf16[4,32,768]{2,1,0:T(8,128)(2,1)} %reduce-scatter.17.cloned.1.call-done), calls=%async_computation.7 | async-start | bytes 393216 | tf_op jit(solution)/shard_map/all_to_all | solution.py:211
  597.8 135.3 %copy-start.4 = (bf16[256,1024]{1,0:T(8,128)(2,1)S(1)}, bf16[256,1024]{1,0:T(8,128)(2,1)}, u32[]{:S(2)}) copy-start(bf16[256,1024]{1,0:T(8,128)(2,1)} %reduce-scatter.13.cloned.1.call-done) | copy-start | bytes 1572868
  597.8 135.3 %copy-start.5 = (bf16[1,256,1024]{2,1,0:T(8,128)(2,1)S(1)}, bf16[1,256,1024]{2,1,0:T(8,128)(2,1)}, u32[]{:S(2)}) copy-start(bf16[1,256,1024]{2,1,0:T(8,128)(2,1)} %param.14) | copy-start | bytes 1572868
Sparse Core Ops, SparseCore 0:
  18.3 45.0 all-gather.12
  89.0 20.0 all-gather.10
  135.2 28.3 reduce-scatter.8
  166.1 49.0 all-gather.16
  217.2 21.0 all-gather.14
  239.7 22.5 all-gather.22
  264.5 49.0 all-gather.18
  325.1 29.6 reduce-scatter.12
  359.2 22.5 all-gather.20
  385.2 68.8 reduce-scatter.20
  457.6 67.3 reduce-scatter.22
  528.3 64.6 reduce-scatter.16
  596.9 61.6 reduce-scatter.18
  660.9 30.1 reduce-scatter.14
  693.5 31.2 reduce-scatter.10
